TPU v7x, 32 devices: a whole 2x2x4 slice. The times are simulated.
32 devices in a mesh: ctx: 16 (over z, x, core), shard: 2 (over y).
Axes of the slice: x: 2, y: 2, z: 4, core: 2. Of those that a mesh axis runs over, the one named last changes fastest.
Arguments:
- tokens: bfloat16 [2, 2048, 1024], P('shard', 'ctx'), may hold values from -64 to 64
- lengths: int32 [2], P('shard'), may hold values from 512 to 2048
- positions: int32 [2, 2048], P('shard', 'ctx'), may hold values from 0 to 1023, as said below
- w_qkv: bfloat16 [1024, 3072], P('shard'), may hold values from -6 to 6
- w_out: bfloat16 [1024, 1024], P('shard'), may hold values from -6 to 6
- w_in: bfloat16 [1024, 5248], P('shard'), may hold values from -0.1875 to 0.1875
- w_down: bfloat16 [2624, 1024], P('shard'), may hold values from -0.125 to 0.125
- gain_attn: bfloat16 [1024], P('shard'), may hold values from 0.25 to 1.75
- gain_mlp: bfloat16 [1024], P('shard'), may hold values from 0.25 to 1.75
- cotangent: bfloat16 [2, 2048, 1024], P('shard', 'ctx'), may hold values from -6 to 6
Outputs:
- output: bfloat16 [2, 2048, 1024], P('shard', 'ctx')
- grad_tokens: float32 [2, 2048, 1024], P('shard', 'ctx')
- grad_qkv: float32 [1024, 3072], P('shard')
- grad_out: float32 [1024, 1024], P('shard')
- grad_in: float32 [1024, 5248], P('shard')
- grad_down: float32 [2624, 1024], P('shard')
- grad_gain_attn: float32 [1024], P('shard')
- grad_gain_mlp: float32 [1024], P('shard')
Inputs may be any that keep to these rules, and one draw needn't show every extreme that they name: Within each sequence positions count up by one from 0 inside documents that follow each other; the first min(1024, 1024) tokens of a sequence form one document, and every token whose index is a multiple of min(1024, 1024) starts a document. The first lengths tokens of a sequence are valid keys, the rest are padding.
All inputs are finite; a program needn't handle non-finite values.
Results may differ from a plain program's by a relative error of at most 0.015.
Values may be sent and summed in bfloat16 or wider, within the bound.
A program may use at most 384 MiB of HBM per device.

v0:
```python
import jax
import jax.numpy as jnp
from jax import lax
from jax.sharding import PartitionSpec as P

HEADS = 16
HEAD_DIM = 64


eps = 1e-05
theta_base = 160000.0
masked_score = -1e30


def layer_norm(value, gain):
    mean = jnp.mean(value, axis=-1, keepdims=True)
    centered = value - mean
    rstd = lax.rsqrt(jnp.mean(centered * centered, axis=-1, keepdims=True) + eps)
    normed = centered * rstd
    return (normed * gain.astype(jnp.float32), normed, rstd)


def norm_back(grad_h, normed, rstd, gain):
    grad_n = grad_h * gain.astype(jnp.float32)
    grad_gain = jnp.sum(grad_h * normed, axis=0)
    grad_x = rstd * (
        grad_n
        - jnp.mean(grad_n, axis=-1, keepdims=True)
        - normed * jnp.mean(grad_n * normed, axis=-1, keepdims=True)
    )
    return (grad_x, grad_gain)


def rope_tables(pos_ids):
    half = HEAD_DIM // 2
    inverse = theta_base ** (-(jnp.arange(half, dtype=jnp.float32) * (2.0 / HEAD_DIM)))
    angles = pos_ids.astype(jnp.float32)[:, None] * inverse[None, :]
    return (jnp.cos(angles)[:, None, :], jnp.sin(angles)[:, None, :])


def rotate(value, cosv, sinv):
    half = value.shape[-1] // 2
    first, second = (value[..., :half], value[..., half:])
    return jnp.concatenate([first * cosv - second * sinv, second * cosv + first * sinv], axis=-1)


def unrotate(value, cosv, sinv):
    half = value.shape[-1] // 2
    first, second = (value[..., :half], value[..., half:])
    return jnp.concatenate([first * cosv + second * sinv, second * cosv - first * sinv], axis=-1)


def gelu_parts(value):
    cdf = 0.5 * (1.0 + jax.scipy.special.erf(value * 0.7071067811865476))
    dens = jnp.exp(-0.5 * value * value) * 0.3989422804014327
    return (value * cdf, cdf + value * dens)


def block_size(total_rows):
    size = total_rows
    while size > 2048 and size % 2 == 0:
        size = size // 2
    return size


def over_blocks(step, carry, pieces, start):
    total_rows = pieces[0].shape[0]
    size = block_size(total_rows)
    turns = total_rows // size
    if turns == 1:
        return step(carry, pieces, start)

    def one_turn(turn, current):
        parts = tuple((lax.dynamic_slice_in_dim(piece, turn * size, size, 0) for piece in pieces))
        return step(current, parts, start + turn * size)

    return lax.fori_loop(0, turns, one_turn, carry)


def shards(tokens, lengths, positions, w_qkv, w_out, w_in, w_down, gain_attn, gain_mlp, cotangent):
    rows = tokens.shape[1]
    width = tokens.shape[2]
    scale = HEAD_DIM ** (-0.5)
    length = lengths[0]
    hidden_in = tokens[0].astype(jnp.float32)
    full_qkv, full_out, full_in, full_down, full_g1, full_g2 = (
        lax.all_gather(w_qkv, "shard", axis=0, tiled=True),
        lax.all_gather(w_out, "shard", axis=0, tiled=True),
        lax.all_gather(w_in, "shard", axis=0, tiled=True),
        lax.all_gather(w_down, "shard", axis=0, tiled=True),
        lax.all_gather(gain_attn, "shard", axis=0, tiled=True),
        lax.all_gather(gain_mlp, "shard", axis=0, tiled=True),
    )
    hidden_units = full_down.shape[0]
    h1, n1, r1 = layer_norm(hidden_in, full_g1)
    hb1 = h1.astype(jnp.bfloat16)
    qkv = jnp.dot(hb1, full_qkv, preferred_element_type=jnp.float32)
    cosv, sinv = rope_tables(positions[0])
    query_heads = rotate(qkv[:, :width].reshape(rows, HEADS, HEAD_DIM), cosv, sinv).astype(
        jnp.bfloat16
    )
    key_heads = rotate(qkv[:, width : 2 * width].reshape(rows, HEADS, HEAD_DIM), cosv, sinv).astype(
        jnp.bfloat16
    )
    value_heads = qkv[:, 2 * width :].reshape(rows, HEADS, HEAD_DIM).astype(jnp.bfloat16)
    key_rows = key_heads.reshape(rows, width)
    value_rows = value_heads.reshape(rows, width)
    query_rows = query_heads.reshape(rows, width)
    key_start = lax.axis_index("ctx") * rows
    key_valid = key_start + jnp.arange(rows) < length

    def forward_step(carry, pieces, start):
        running, total, accum = carry
        key_piece, value_piece = pieces
        count = key_piece.shape[0]
        key_part = key_piece.reshape(count, HEADS, HEAD_DIM)
        value_part = value_piece.reshape(count, HEADS, HEAD_DIM)
        valid = start + jnp.arange(count) < length
        scores = (
            jnp.einsum("qhd,khd->hqk", query_heads, key_part, preferred_element_type=jnp.float32)
            * scale
        )
        scores = jnp.where(valid, scores, masked_score)
        newest = jnp.maximum(running, jnp.max(scores, axis=-1))
        factor = jnp.exp(running - newest)
        expo = jnp.where(valid, jnp.exp(scores - newest[:, :, None]), 0.0)
        total = total * factor + jnp.sum(expo, axis=-1)
        accum = accum * factor[:, :, None] + jnp.einsum(
            "hqk,khd->hqd",
            expo.astype(jnp.bfloat16),
            value_part,
            preferred_element_type=jnp.float32,
        )
        return (newest, total, accum)

    start_state = (
        jnp.full((HEADS, rows), masked_score, jnp.float32),
        jnp.zeros((HEADS, rows), jnp.float32),
        jnp.zeros((HEADS, rows, HEAD_DIM), jnp.float32),
    )
    running, total, accum = over_blocks(
        forward_step,
        start_state,
        (
            lax.all_gather(key_rows, "ctx", axis=0, tiled=True),
            lax.all_gather(value_rows, "ctx", axis=0, tiled=True),
        ),
        jnp.int32(0),
    )
    attended = jnp.transpose(accum / total[:, :, None], (1, 0, 2))
    lse_local = running + jnp.log(total)
    ob = attended.reshape(rows, width).astype(jnp.bfloat16)
    mid = hidden_in + jnp.dot(ob, full_out, preferred_element_type=jnp.float32)
    h2, n2, r2 = layer_norm(mid, full_g2)
    hb2 = h2.astype(jnp.bfloat16)
    u = jnp.dot(hb2, full_in, preferred_element_type=jnp.float32)
    inp, gate = (u[:, :hidden_units], u[:, hidden_units:])
    gel, dgel = gelu_parts(inp)
    act = (gel * gate).astype(jnp.bfloat16)
    output = (mid + jnp.dot(act, full_down, preferred_element_type=jnp.float32)).astype(
        jnp.bfloat16
    )
    cot_b = cotangent[0]
    d_act = jnp.dot(cot_b, full_down.T, preferred_element_type=jnp.float32)
    d_u = jnp.concatenate([d_act * gate * dgel, d_act * gel], axis=1).astype(jnp.bfloat16)
    d_h2 = jnp.dot(d_u, full_in.T, preferred_element_type=jnp.float32)
    d_x2, grad_g2 = norm_back(d_h2, n2, r2, full_g2)
    d_mid = cot_b.astype(jnp.float32) + d_x2
    d_mid_b = d_mid.astype(jnp.bfloat16)
    grad_rows = jnp.dot(d_mid_b, full_out.T, preferred_element_type=jnp.float32).astype(
        jnp.bfloat16
    )
    grad_heads = grad_rows.reshape(rows, HEADS, HEAD_DIM)
    delta_local = jnp.transpose(jnp.sum(grad_heads.astype(jnp.float32) * attended, axis=-1))
    lse_all, delta_all = (
        lax.all_gather(lse_local, "ctx", axis=1, tiled=True),
        lax.all_gather(delta_local, "ctx", axis=1, tiled=True),
    )

    def query_step(grad_q, pieces, start):
        key_piece, value_piece = pieces
        count = key_piece.shape[0]
        key_part = key_piece.reshape(count, HEADS, HEAD_DIM)
        value_part = value_piece.reshape(count, HEADS, HEAD_DIM)
        valid = start + jnp.arange(count) < length
        scores = (
            jnp.einsum("qhd,khd->hqk", query_heads, key_part, preferred_element_type=jnp.float32)
            * scale
        )
        probs = jnp.where(valid, jnp.exp(scores - lse_local[:, :, None]), 0.0)
        grad_p = jnp.einsum(
            "qhd,khd->hqk", grad_heads, value_part, preferred_element_type=jnp.float32
        )
        grad_s = (probs * (grad_p - delta_local[:, :, None])).astype(jnp.bfloat16)
        return grad_q + jnp.einsum(
            "hqk,khd->qhd", grad_s, key_part, preferred_element_type=jnp.float32
        )

    def key_step(carry, pieces, start):
        grad_k, grad_v = carry
        query_piece, grad_piece = pieces
        count = query_piece.shape[0]
        query_part = query_piece.reshape(count, HEADS, HEAD_DIM)
        grad_part = grad_piece.reshape(count, HEADS, HEAD_DIM)
        lse_part = lax.dynamic_slice_in_dim(lse_all, start, count, 1)
        delta_part = lax.dynamic_slice_in_dim(delta_all, start, count, 1)
        scores = (
            jnp.einsum("qhd,khd->hqk", query_part, key_heads, preferred_element_type=jnp.float32)
            * scale
        )
        probs = jnp.where(key_valid, jnp.exp(scores - lse_part[:, :, None]), 0.0)
        grad_v = grad_v + jnp.einsum(
            "hqk,qhd->khd",
            probs.astype(jnp.bfloat16),
            grad_part,
            preferred_element_type=jnp.float32,
        )
        grad_p = jnp.einsum(
            "qhd,khd->hqk", grad_part, value_heads, preferred_element_type=jnp.float32
        )
        grad_s = (probs * (grad_p - delta_part[:, :, None])).astype(jnp.bfloat16)
        grad_k = grad_k + jnp.einsum(
            "hqk,qhd->khd", grad_s, query_part, preferred_element_type=jnp.float32
        )
        return (grad_k, grad_v)

    zero_heads = jnp.zeros((rows, HEADS, HEAD_DIM), jnp.float32)
    grad_q = over_blocks(
        query_step,
        zero_heads,
        (
            lax.all_gather(key_rows, "ctx", axis=0, tiled=True),
            lax.all_gather(value_rows, "ctx", axis=0, tiled=True),
        ),
        jnp.int32(0),
    )
    grad_k, grad_v = over_blocks(
        key_step,
        (zero_heads, zero_heads),
        (
            lax.all_gather(query_rows, "ctx", axis=0, tiled=True),
            lax.all_gather(grad_rows, "ctx", axis=0, tiled=True),
        ),
        jnp.int32(0),
    )
    grad_q = unrotate(grad_q * scale, cosv, sinv)
    grad_k = unrotate(grad_k * scale, cosv, sinv)
    d_qkv = jnp.concatenate(
        [grad_q.reshape(rows, width), grad_k.reshape(rows, width), grad_v.reshape(rows, width)],
        axis=1,
    ).astype(jnp.bfloat16)
    d_h1 = jnp.dot(d_qkv, full_qkv.T, preferred_element_type=jnp.float32)
    d_x1, grad_g1 = norm_back(d_h1, n1, r1, full_g1)
    grad_tokens = d_mid + d_x1
    grad_qkv = jnp.dot(hb1.T, d_qkv, preferred_element_type=jnp.float32)
    grad_out = jnp.dot(ob.T, d_mid_b, preferred_element_type=jnp.float32)
    grad_in = jnp.dot(hb2.T, d_u, preferred_element_type=jnp.float32)
    grad_down = jnp.dot(act.T, cot_b, preferred_element_type=jnp.float32)
    shares = (
        lax.psum_scatter(grad_qkv, "shard", scatter_dimension=0, tiled=True),
        lax.psum_scatter(grad_out, "shard", scatter_dimension=0, tiled=True),
        lax.psum_scatter(grad_in, "shard", scatter_dimension=0, tiled=True),
        lax.psum_scatter(grad_down, "shard", scatter_dimension=0, tiled=True),
        lax.psum_scatter(grad_g1, "shard", scatter_dimension=0, tiled=True),
        lax.psum_scatter(grad_g2, "shard", scatter_dimension=0, tiled=True),
    )
    summed = lax.psum((shares[0], shares[1], shares[2], shares[3], shares[4], shares[5]), "ctx")
    return (
        output.reshape(1, rows, width),
        grad_tokens.reshape(1, rows, width),
        summed[0],
        summed[1],
        summed[2],
        summed[3],
        summed[4],
        summed[5],
    )


def solution(mesh):
    in_specs = (
        P("shard", "ctx", None),
        P("shard"),
        P("shard", "ctx"),
        P("shard", None),
        P("shard", None),
        P("shard", None),
        P("shard", None),
        P("shard"),
        P("shard"),
        P("shard", "ctx", None),
    )
    out_specs = (
        P("shard", "ctx", None),
        P("shard", "ctx", None),
        P("shard", None),
        P("shard", None),
        P("shard", None),
        P("shard", None),
        P("shard"),
        P("shard"),
    )
    return jax.shard_map(shards, mesh=mesh, in_specs=in_specs, out_specs=out_specs, check_vma=False)
```

profile of v0, /device:TPU:0, one launch (start us, length us, event | category | flops | bytes accessed | tf_op | source)
XLA Modules:
  0.0 1579.1 jit_solution(17949606483636141829)
XLA Ops:
  8.6 5.3 all-gather
  13.9 1.1 convert_reduce_fusion
  15.0 1.2 fusion.57
  16.2 76.4 %all-gather.11.cloned.1.call-done = bf16[1024,3072]{1,0:T(8,128)(2,1)} async-done(((bf16[512,3072]{1,0:T(8,128)(2,1)}), bf16[1024,3072]{1,0:T(8,128)(2,1)}) %all-gather.11.cloned.1.call-update) | async-done | bytes 6291472 | tf_op jit(solution)/shard_map/all_gather | solution.py:87
  92.6 4.0 fusion.82
  102.2 4.4 all-gather.1
  107.4 40.5 %all-gather.15.cloned.1.call-done = bf16[2048,1024]{1,0:T(8,128)(2,1)} async-done(((bf16[128,1024]{1,0:T(8,128)(2,1)}), bf16[2048,1024]{1,0:T(8,128)(2,1)}) %all-gather.15.cloned.1.call-update) | async-done | bytes 4194320 | tf_op jit(solution)/shard_map/all_gather | solution.py:146
  147.9 6.4 copy.37
  154.3 47.4 %all-gather.13.cloned.1.call-done = bf16[2048,1024]{0,1:T(8,128)(2,1)} async-done(((bf16[128,1024]{0,1:T(8,128)(2,1)}), bf16[2048,1024]{0,1:T(8,128)(2,1)}) %all-gather.13.cloned.1.call-update) | async-done | bytes 4194320 | tf_op jit(solution)/shard_map/all_gather | solution.py:145
  201.7 4.4 select_reduce_fusion
  206.1 4.5 fusion.1
  210.6 2.1 copy-done
  212.8 11.9 fusion.86
  224.7 9.7 all-gather.17.cloned.1.call-done
  234.4 2.1 fusion.87
  236.8 131.4 %all-gather.19.cloned.1.call-done = bf16[1024,5248]{1,0:T(8,128)(2,1)} async-done(((bf16[512,5248]{1,0:T(8,128)(2,1)}), bf16[1024,5248]{1,0:T(8,128)(2,1)}) %all-gather.19.cloned.1.call-update) | async-done | bytes 10747920 | tf_op jit(solution)/shard_map/all_gather | solution.py:89
  368.2 5.7 fusion.84
  373.9 65.7 %all-gather.21.cloned.1.call-done = bf16[2624,1024]{1,0:T(8,128)(2,1)} async-done(((bf16[1312,1024]{1,0:T(8,128)(2,1)}), bf16[2624,1024]{1,0:T(8,128)(2,1)}) %all-gather.21.cloned.1.call-update) | async-done | bytes 5373968 | tf_op jit(solution)/shard_map/all_gather | solution.py:90
  439.6 4.6 fusion.22
  444.3 8.3 multiply_reduce_fusion
  452.9 1.5 convolution_convert_fusion
  454.5 2.7 fusion.64
  457.5 7.7 fusion.60
  466.5 22.8 %all_gather.47 = f32[16,2048]{1,0:T(8,128)S(1)} all-gather(f32[16,128]{1,0:T(8,128)S(1)} %get-tuple-element.38), channel_id=1, replica_groups=mesh['ctx'=16,'shard'=2] {'ctx'}, dimensions={1}, use_global_device_ids=true | all-gather | bytes 139264 | tf_op jit(solution)/shard_map/all_gather | solution.py:176
  489.4 17.8 %all_gather.49 = f32[16,2048]{1,0:T(8,128)S(1)} all-gather(f32[16,128]{1,0:T(8,128)S(1)} %bitcast.151), channel_id=1, replica_groups=mesh['ctx'=16,'shard'=2] {'ctx'}, dimensions={1}, use_global_device_ids=true | all-gather | bytes 139264 | tf_op jit(solution)/shard_map/all_gather | solution.py:177
  507.2 10.4 fusion.88
  517.6 12.6 fusion.32
  530.2 16.6 %all-gather.25.cloned.1.call-done = bf16[2048,1024]{1,0:T(8,128)(2,1)} async-done(((bf16[128,1024]{1,0:T(8,128)(2,1)}), bf16[2048,1024]{1,0:T(8,128)(2,1)}) %all-gather.25.cloned.1.call-update) | async-done | bytes 4194320 | tf_op jit(solution)/shard_map/all_gather | solution.py:242
  546.8 6.4 copy.41
  553.3 15.1 multiply_convert_fusion.21
  568.4 1.6 fusion.30
  570.8 8.4 fusion.33
  579.2 6.5 fusion.58
  585.7 1.0 copy-done.16
  587.0 9.0 fusion.41
  596.3 6.4 reduce-scatter.7.cloned.1.call-done
  602.6 127.5 %reduce-scatter.11.cloned.1.call-done = f32[1312,1024]{1,0:T(8,128)} async-done(((f32[2624,1024]{1,0:T(8,128)}), f32[1312,1024]{1,0:T(8,128)}) %reduce-scatter.11.cloned.1.call-update) | async-done | bytes 5373968 | tf_op jit(solution)/shard_map/reduce_scatter | solution.py:263
  730.2 146.9 %reduce-scatter.5.cloned.1.call-done = f32[512,3072]{1,0:T(8,128)} async-done(((f32[1024,3072]{1,0:T(8,128)}), f32[512,3072]{1,0:T(8,128)}) %reduce-scatter.5.cloned.1.call-update) | async-done | bytes 6291472 | tf_op jit(solution)/shard_map/reduce_scatter | solution.py:260
  877.1 242.1 %reduce-scatter.9.cloned.1.call-done = f32[512,5248]{1,0:T(8,128)} async-done(((f32[1024,5248]{1,0:T(8,128)}), f32[512,5248]{1,0:T(8,128)}) %reduce-scatter.9.cloned.1.call-update) | async-done | bytes 10747920 | tf_op jit(solution)/shard_map/reduce_scatter | solution.py:262
  1121.1 5.2 fusion.37
  1126.3 5.1 fusion.56
  1131.4 5.0 all-reduce.4
  1136.5 34.5 %all-reduce.2 = (f32[512]{0:T(512)}, f32[512]{0:T(512)}) all-reduce(f32[512]{0:T(512)S(1)} %dynamic-slice.1, f32[512]{0:T(512)S(1)} %dynamic-slice.3), channel_id=1, replica_groups=mesh['ctx'=16,'shard'=2] {'ctx'}, use_global_device_ids=true, to_apply=%region_21.22 | all-reduce | flops 1024 | bytes 8192 | tf_op jit(solution)/shard_map/psum | solution.py:267
  1172.1 379.7 %all-reduce.7.cloned.1.call-done = (f32[512,3072]{1,0:T(8,128)}, f32[512,1024]{1,0:T(8,128)}, f32[512,5248]{1,0:T(8,128)}, f32[1312,1024]{1,0:T(8,128)}) async-done(((f32[512,3072]{1,0:T(8,128)}, f32[512,1024]{1,0:T(8,128)}, f32[512,5248]{1,0:T(8,128)}, f32[1312,1024]{1,0:T(8,128)}), (f32[512,3072]{1,0:T(8,128)}, f32[512,1024]{1,0:T(8,128)}, f32[512,5248]{1,0:T(8,128)}, ...) | async-done | bytes 24510480 | tf_op jit(solution)/shard_map/psum | solution.py:267
  1551.9 6.9 copy.49
  1558.7 3.4 copy.50
  1562.2 4.2 copy.51
  1566.3 5.8 copy.52
  (118 shorter events, 13.1 us)
Async XLA Ops:
  7.2 85.5 %all-gather.11.cloned.1.call-start = ((), (), s32[]{:S(2)}) async-start(), calls=%async_computation.4 | async-start | bytes 9437184 | tf_op jit(solution)/shard_map/all_gather | solution.py:87
  7.9 140.0 %all-gather.15.cloned.1.call-start = ((), (), s32[]{:S(2)}) async-start(), calls=%async_computation.6 | async-start | bytes 4456448 | tf_op jit(solution)/shard_map/all_gather | solution.py:146
  92.6 4.8 copy-start.21
  97.4 104.3 %all-gather.13.cloned.1.call-start = ((), (), s32[]{:S(2)}) async-start(), calls=%async_computation.5 | async-start | bytes 4456448 | tf_op jit(solution)/shard_map/all_gather | solution.py:145
  98.3 0.7 copy-start.8
  98.3 1.4 copy-start.10
  99.7 134.7 %all-gather.17.cloned.1.call-start = ((), (), s32[]{:S(2)}) async-start(), calls=%async_computation.7 | async-start | bytes 3145728 | tf_op jit(solution)/shard_map/all_gather | solution.py:88
  100.3 1.9 copy-start.20
  100.3 267.9 %all-gather.19.cloned.1.call-start = ((), (), s32[]{:S(2)}) async-start(), calls=%async_computation.8 | async-start | bytes 16121856 | tf_op jit(solution)/shard_map/all_gather | solution.py:89
  100.9 338.8 %all-gather.21.cloned.1.call-start = ((), (), s32[]{:S(2)}) async-start(), calls=%async_computation.9 | async-start | bytes 8060928 | tf_op jit(solution)/shard_map/all_gather | solution.py:90
  101.4 405.7 %all-gather.23.cloned.1.call-start = ((), (), s32[]{:S(2)}) async-start(), calls=%async_computation.10 | async-start | bytes 4456448 | tf_op jit(solution)/shard_map/all_gather | solution.py:241
  107.3 439.5 %all-gather.25.cloned.1.call-start = ((), (), s32[]{:S(2)}) async-start(), calls=%async_computation.11 | async-start | bytes 4456448 | tf_op jit(solution)/shard_map/all_gather | solution.py:242
  206.1 6.6 copy-start
  212.7 21.6 %copy-start.2 = (bf16[1,128,1024]{2,1,0:T(8,128)(2,1)S(1)}, bf16[1,128,1024]{2,1,0:T(8,128)(2,1)}, u32[]{:S(2)}) copy-start(bf16[1,128,1024]{2,1,0:T(8,128)(2,1)} %param.10) | copy-start | bytes 786436
  224.7 143.5 %copy-start.13 = (bf16[128,16,64]{0,2,1:T(8,128)(2,1)}, bf16[128,16,64]{0,2,1:T(8,128)(2,1)S(1)}, u32[]{:S(2)}) copy-start(bf16[128,16,64]{0,2,1:T(8,128)(2,1)S(1)} %get-tuple-element.44) | copy-start | bytes 786436
  373.9 70.3 %copy-start.5 = (f32[128,5248]{1,0:T(8,128)}, f32[128,5248]{1,0:T(8,128)S(1)}, u32[]{:S(2)}) copy-start(f32[128,5248]{1,0:T(8,128)S(1)} %fusion.84) | copy-start | bytes 8060932
  444.3 8.3 copy-start.15
  444.3 8.3 copy-start.17
  444.3 8.3 copy-start.12
  444.3 8.6 copy-start.4
  452.6 1.9 copy-start.14
  454.5 148.2 %reduce-scatter.7.cloned.1.call-start = ((), (), s32[]{:S(2)}) async-start(), calls=%async_computation.13 | async-start | bytes 6291456 | tf_op jit(solution)/shard_map/reduce_scatter | solution.py:261
  457.3 272.9 %reduce-scatter.11.cloned.1.call-start = ((), (), s32[]{:S(2)}) async-start(), calls=%async_computation.15 | async-start | bytes 16121856 | tf_op jit(solution)/shard_map/reduce_scatter | solution.py:263
  465.2 0.9 copy-start.6
  465.2 1.1 copy-start.7
  465.2 24.1 %copy-start.19 = (f32[128,16,64]{0,2,1:T(8,128)S(1)}, f32[128,16,64]{0,2,1:T(8,128)}, u32[]{:S(2)}) copy-start(f32[128,16,64]{0,2,1:T(8,128)} %get-tuple-element.45) | copy-start | bytes 1572868
  465.2 41.9 %copy-start.9 = (bf16[128,16,32]{0,2,1:T(8,128)(2,1)S(1)}, bf16[128,16,32]{0,2,1:T(8,128)(2,1)}, u32[]{:S(2)}) copy-start(bf16[128,16,32]{0,2,1:T(8,128)(2,1)} %copy-done.8) | copy-start | bytes 393220
  465.3 41.9 %copy-start.11 = (bf16[128,16,32]{0,2,1:T(8,128)(2,1)S(1)}, bf16[128,16,32]{0,2,1:T(8,128)(2,1)}, u32[]{:S(2)}) copy-start(bf16[128,16,32]{0,2,1:T(8,128)(2,1)} %copy-done.10) | copy-start | bytes 393220
  465.3 411.8 %reduce-scatter.5.cloned.1.call-start = ((), (), s32[]{:S(2)}) async-start(), calls=%async_computation.12 | async-start | bytes 18874368 | tf_op jit(solution)/shard_map/reduce_scatter | solution.py:260
  553.3 15.1 copy-start.1
  553.3 16.9 %slice-start = ((s8[16777216]{0:T(1024)(128)(4,1)}), s8[4194304]{0:T(1024)(128)(4,1)S(1)}, s32[]{:S(2)}) async-start(s8[16777216]{0:T(1024)(128)(4,1)} %bitcast.121), calls=%async_computation.17 | async-start | bytes 8388608
  553.3 16.9 %slice-start.1 = ((s8[16777216]{0:T(1024)(128)(4,1)}), s8[4194304]{0:T(1024)(128)(4,1)S(1)}, s32[]{:S(2)}) async-start(s8[16777216]{0:T(1024)(128)(4,1)} %bitcast.121), calls=%async_computation.18 | async-start | bytes 8388608
  553.3 16.9 %slice-start.2 = ((s8[16777216]{0:T(1024)(128)(4,1)}), s8[4194304]{0:T(1024)(128)(4,1)S(1)}, s32[]{:S(2)}) async-start(s8[16777216]{0:T(1024)(128)(4,1)} %bitcast.121), calls=%async_computation.19 | async-start | bytes 8388608
  568.3 2.4 slice-start.3
  585.7 1.1 copy-start.16
  585.7 1.3 copy-start.18
  585.7 533.5 %reduce-scatter.9.cloned.1.call-start = ((), (), s32[]{:S(2)}) async-start(), calls=%async_computation.14 | async-start | bytes 32243712 | tf_op jit(solution)/shard_map/reduce_scatter | solution.py:262
  596.0 955.9 %all-reduce.7.cloned.1.call-start = ((), (), s32[]{:S(2)}) async-start(), calls=%async_computation.16 | async-start | bytes 49020928 | tf_op jit(solution)/shard_map/psum | solution.py:267
  1119.2 0.7 copy-start.22
  1551.8 10.3 copy-start.3
Sparse Core Ops, SparseCore 0:
  9.5 83.0 all-gather.10
  97.5 50.3 all-gather.14
  150.6 51.0 all-gather.12
  203.1 31.2 all-gather.16
  235.8 132.3 all-gather.18
  369.6 70.0 all-gather.20
  441.8 53.8 all-gather.22
  498.4 48.4 all-gather.24
  549.7 52.8 reduce-scatter.6
  605.4 124.7 reduce-scatter.10
  732.5 144.5 reduce-scatter.4
  879.2 239.9 reduce-scatter.8
  1124.1 427.7 all-reduce.6
where the time goes:
time: 1580 us
  waiting for transfers between devices  1290 us (82%)
  matrix products  127 us (8%)
  blocking collectives  89.8 us (6%)
  local copies, waits for them, and re-layouts  42.3 us (3%)
  between operations  16.1 us (1%)
    psum x1, waiting for transfers between devices, shards(): lax.psum((shares[0], shares[1], shares[2], shares[3], shares[4], shares[5...  380 us
    reduce_scatter x1, waiting for transfers between devices, shards(): lax.psum_scatter(grad_in, 'shard', scatter_dimension=0, tiled=True)  242 us
    reduce_scatter x1, waiting for transfers between devices, shards(): lax.psum_scatter(grad_qkv, 'shard', scatter_dimension=0, tiled=True)  147 us
    all_gather x1, waiting for transfers between devices, shards(): lax.all_gather(w_in, 'shard', axis=0, tiled=True)  131 us
    reduce_scatter x1, waiting for transfers between devices, shards(): lax.psum_scatter(grad_down, 'shard', scatter_dimension=0, tiled=True)  128 us
    all_gather x1, waiting for transfers between devices, shards(): lax.all_gather(w_qkv, 'shard', axis=0, tiled=True)  76.4 us
    all_gather x1, waiting for transfers between devices, shards(): lax.all_gather(w_down, 'shard', axis=0, tiled=True)  65.7 us
    all_gather x1, waiting for transfers between devices, shards(): lax.all_gather(key_rows, 'ctx', axis=0, tiled=True)  47.4 us
  transfers between devices with their start and end apart: 13, of which 12 were waited for; matrix products, arithmetic and copies ran while one was open for 9% of the time, Pallas kernels for 0%

commit v1 on v0

--- a/solution.py
+++ b/solution.py
@@ -1,6 +1,10 @@
+import functools
+
 import jax
 import jax.numpy as jnp
 from jax import lax
+from jax.experimental import pallas as pl
+from jax.experimental.pallas import tpu as pltpu
 from jax.sharding import PartitionSpec as P
 
 HEADS = 16
@@ -277,6 +281,474 @@
     )
 
 
+MESH = pl.DeviceIdType.MESH
+F32 = jnp.float32
+BF16 = jnp.bfloat16
+CTX = 16
+
+
+def fast_fits(mesh):
+    return mesh.shape["ctx"] == CTX and mesh.shape["shard"] == 2
+
+
+def place():
+    me = lax.axis_index("ctx")
+    return me, me // 4, (me // 2) % 2, me % 2
+
+
+def at(z, x, c):
+    return {"ctx": z * 4 + x * 2 + c}
+
+
+def when(cond, body):
+    if cond is True:
+        body()
+    else:
+        pl.when(cond)(body)
+
+
+def both(a, b):
+    if a is True:
+        return b
+    if b is True:
+        return a
+    return jnp.logical_and(a, b)
+
+
+def gather_kernel(sources, count, *refs):
+    ins, outs = refs[:count], refs[count : 2 * count]
+    local_sem, send_sem, recv_sem = refs[2 * count :]
+    me, z, x, c = place()
+    y = lax.axis_index("shard")
+    up, down = z < 3, z > 0
+    barrier = pltpu.get_barrier_semaphore()
+    when(up, lambda: pl.semaphore_signal(barrier, 1, device_id=at(z + 1, x, c), device_id_type=MESH))
+    when(down, lambda: pl.semaphore_signal(barrier, 1, device_id=at(z - 1, x, c), device_id_type=MESH))
+    pl.semaphore_signal(barrier, 1, device_id=at(z, 1 - x, c), device_id_type=MESH)
+    pl.semaphore_signal(barrier, 1, device_id=at(z, x, 1 - c), device_id_type=MESH)
+    pl.semaphore_wait(barrier, 2 + up.astype(jnp.int32) + down.astype(jnp.int32))
+    targets = (at(z + 1, x, c), at(z - 1, x, c), at(z, 1 - x, c), at(z, x, 1 - c))
+
+    def has(a, zo):
+        return sources[a](zo, y)
+
+    def copy(a, src, origin, way):
+        return pltpu.make_async_remote_copy(
+            src_ref=src,
+            dst_ref=outs[a].at[origin],
+            send_sem=send_sem.at[a, way, origin],
+            recv_sem=recv_sem.at[a, origin],
+            device_id=targets[way],
+            device_id_type=MESH,
+        )
+
+    def got(a, origin):
+        copy(a, ins[a], origin, 3).wait_recv()
+
+    def own(a):
+        def go():
+            pltpu.make_async_copy(ins[a], outs[a].at[me], local_sem.at[a]).start()
+            when(up, lambda: copy(a, ins[a], me, 0).start())
+            when(down, lambda: copy(a, ins[a], me, 1).start())
+            copy(a, ins[a], me, 2).start()
+            copy(a, ins[a], me, 3).start()
+
+        when(has(a, z), go)
+
+    for a in range(count):
+        own(a)
+    for d in (1, 2, 3):
+        for a in range(count):
+
+            def below(a=a, zo=z - d):
+                origin = zo * 4 + x * 2 + c
+                got(a, origin)
+                when(up, lambda: copy(a, outs[a].at[origin], origin, 0).start())
+                copy(a, outs[a].at[origin], origin, 2).start()
+                copy(a, outs[a].at[origin], origin, 3).start()
+
+            def above(a=a, zo=z + d):
+                origin = zo * 4 + x * 2 + c
+                got(a, origin)
+                when(down, lambda: copy(a, outs[a].at[origin], origin, 1).start())
+                copy(a, outs[a].at[origin], origin, 2).start()
+                copy(a, outs[a].at[origin], origin, 3).start()
+
+            when(both(has(a, z - d), z - d >= 0), below)
+            when(both(has(a, z + d), z + d <= 3), above)
+    for k in range(4):
+        zo = lax.rem(z + k, 4)
+        origin = zo * 4 + (1 - x) * 2 + c
+        for a in range(count):
+
+            def across(a=a, origin=origin):
+                got(a, origin)
+                copy(a, outs[a].at[origin], origin, 3).start()
+
+            when(has(a, zo), across)
+    for k in range(8):
+        zo = k // 2
+        for a in range(count):
+            when(has(a, zo), lambda a=a, k=k: got(a, k * 2 + 1 - c))
+    for a in range(count):
+        when(has(a, z), lambda a=a: pltpu.make_async_copy(ins[a], outs[a].at[me], local_sem.at[a]).wait())
+        for zo in range(4):
+            origin = zo * 4 + x * 2 + c
+            other = zo * 4 + (1 - x) * 2 + c
+
+            def drain(a=a, zo=zo, origin=origin, other=other):
+                when(both(up, zo <= z), lambda: copy(a, ins[a], origin, 0).wait_send())
+                when(both(down, zo >= z), lambda: copy(a, ins[a], origin, 1).wait_send())
+                copy(a, ins[a], origin, 2).wait_send()
+                copy(a, ins[a], origin, 3).wait_send()
+                copy(a, ins[a], other, 3).wait_send()
+
+            when(has(a, zo), drain)
+
+
+def everywhere(zo, y):
+    return True
+
+
+def gather(arrays, cid, name, sources=None):
+    count = len(arrays)
+    sources = sources or (everywhere,) * count
+    kernel = functools.partial(gather_kernel, sources, count)
+    hbm = pl.BlockSpec(memory_space=pl.ANY)
+    return pl.pallas_call(
+        kernel,
+        out_shape=[jax.ShapeDtypeStruct((CTX,) + a.shape, a.dtype) for a in arrays],
+        in_specs=[hbm] * count,
+        out_specs=[hbm] * count,
+        scratch_shapes=[
+            pltpu.SemaphoreType.DMA((count,)),
+            pltpu.SemaphoreType.DMA((count, 4, CTX)),
+            pltpu.SemaphoreType.DMA((count, CTX)),
+        ],
+        compiler_params=pltpu.CompilerParams(collective_id=cid, has_side_effects=True),
+        name=name,
+    )(*arrays)
+
+
+def exchange_kernel(peers, spread, in_ref, out_ref, local_sem, send_sem, recv_sem):
+    members, mine = peers()
+    size = len(members)
+    barrier = pltpu.get_barrier_semaphore()
+    for k in range(1, size):
+        pl.semaphore_signal(barrier, 1, device_id={"ctx": members[k][0]}, device_id_type=MESH)
+    pl.semaphore_wait(barrier, size - 1)
+
+    def source(slot):
+        return in_ref if spread else in_ref.at[slot]
+
+    def copy(k, dst):
+        device, slot = members[k]
+        return pltpu.make_async_remote_copy(
+            src_ref=source(slot),
+            dst_ref=out_ref.at[dst],
+            send_sem=send_sem.at[k],
+            recv_sem=recv_sem.at[dst],
+            device_id={"ctx": device},
+            device_id_type=MESH,
+        )
+
+    local = pltpu.make_async_copy(source(mine), out_ref.at[mine], local_sem)
+    for k in range(1, size):
+        copy(k, mine).start()
+    local.start()
+    local.wait()
+    for k in range(1, size):
+        arrived = copy(k, members[k][1])
+        arrived.wait_recv()
+        arrived.wait_send()
+
+
+def exchange(array, peers, size, cid, name, spread=False):
+    shape = ((size,) + array.shape) if spread else array.shape
+    hbm = pl.BlockSpec(memory_space=pl.ANY)
+    return pl.pallas_call(
+        functools.partial(exchange_kernel, peers, spread),
+        out_shape=jax.ShapeDtypeStruct(shape, array.dtype),
+        in_specs=[hbm],
+        out_specs=hbm,
+        scratch_shapes=[
+            pltpu.SemaphoreType.DMA,
+            pltpu.SemaphoreType.DMA((size,)),
+            pltpu.SemaphoreType.DMA((size,)),
+        ],
+        compiler_params=pltpu.CompilerParams(collective_id=cid, has_side_effects=True),
+        name=name,
+    )(array)
+
+
+def all_peers():
+    me = lax.axis_index("ctx")
+    return [(lax.rem(me + k, CTX), lax.rem(me + k, CTX)) for k in range(CTX)], me
+
+
+def square_peers():
+    me, z, x, c = place()
+    corner, zp = (z // 2) * 2, z % 2
+    members = []
+    for dz, dx in ((0, 0), (0, 1), (1, 0), (1, 1)):
+        oz, ox = (zp + dz) % 2, (x + dx) % 2
+        members.append(((corner + oz) * 4 + ox * 2 + c, oz * 2 + ox))
+    return members, zp * 2 + x
+
+
+BQ = 256
+
+
+def attend_kernel(len_ref, k_ref, q_ref, v_ref, o_ref, lse_ref):
+    total_keys = k_ref.shape[0]
+    length = len_ref[0]
+    valid = lax.broadcasted_iota(jnp.int32, (total_keys, BQ), 0) < length
+
+    def step(i, carry):
+        cols = pl.ds(pl.multiple_of(i * BQ, BQ), BQ)
+        s = jnp.dot(k_ref[...], q_ref[:, cols], preferred_element_type=F32)
+        s = jnp.where(valid, s, masked_score)
+        top = jnp.max(s, axis=0, keepdims=True)
+        e = jnp.exp(s - top)
+        tot = jnp.sum(e, axis=0, keepdims=True)
+        acc = jnp.dot(v_ref[...], e.astype(BF16), preferred_element_type=F32)
+        o_ref[:, cols] = acc / tot
+        lse_ref[:, cols] = top + jnp.log(tot)
+        return carry
+
+    lax.fori_loop(0, total_keys // BQ, step, 0)
+
+
+def attend(length, k_nat, q_t, v_t):
+    keys = k_nat.shape[0]
+    vmem = pl.BlockSpec(memory_space=pltpu.VMEM)
+    return pl.pallas_call(
+        attend_kernel,
+        out_shape=(
+            jax.ShapeDtypeStruct((HEAD_DIM, keys), F32),
+            jax.ShapeDtypeStruct((1, keys), F32),
+        ),
+        in_specs=[pl.BlockSpec(memory_space=pltpu.SMEM), vmem, vmem, vmem],
+        out_specs=(vmem, vmem),
+        name="attend",
+    )(length, k_nat, q_t, v_t)
+
+
+def attend_back_kernel(
+    len_ref, k_ref, v_ref, kt_ref, q_ref, qn_ref, do_ref, don_ref, lse_ref, delta_ref, dq_ref, dk_ref, dv_ref
+):
+    total_keys = k_ref.shape[0]
+    length = len_ref[0]
+    valid = lax.broadcasted_iota(jnp.int32, (total_keys, BQ), 0) < length
+    dk_ref[...] = jnp.zeros_like(dk_ref)
+    dv_ref[...] = jnp.zeros_like(dv_ref)
+
+    def step(i, carry):
+        cols = pl.ds(pl.multiple_of(i * BQ, BQ), BQ)
+        s = jnp.dot(k_ref[...], q_ref[:, cols], preferred_element_type=F32)
+        p = jnp.where(valid, jnp.exp(s - lse_ref[:, cols]), 0.0)
+        dp = jnp.dot(v_ref[...], do_ref[:, cols], preferred_element_type=F32)
+        ds = (p * (dp - delta_ref[:, cols])).astype(BF16)
+        dq_ref[:, cols] = jnp.dot(kt_ref[...], ds, preferred_element_type=F32)
+        dk_ref[...] += jnp.dot(ds, qn_ref[cols, :], preferred_element_type=F32)
+        dv_ref[...] += jnp.dot(p.astype(BF16), don_ref[cols, :], preferred_element_type=F32)
+        return carry
+
+    lax.fori_loop(0, total_keys // BQ, step, 0)
+
+
+def attend_back(length, k_nat, v_nat, k_t, q_t, q_nat, do_t, do_nat, lse, delta):
+    keys = k_nat.shape[0]
+    vmem = pl.BlockSpec(memory_space=pltpu.VMEM)
+    return pl.pallas_call(
+        attend_back_kernel,
+        out_shape=(
+            jax.ShapeDtypeStruct((HEAD_DIM, keys), F32),
+            jax.ShapeDtypeStruct((keys, HEAD_DIM), F32),
+            jax.ShapeDtypeStruct((keys, HEAD_DIM), F32),
+        ),
+        in_specs=[pl.BlockSpec(memory_space=pltpu.SMEM)] + [vmem] * 9,
+        out_specs=(vmem, vmem, vmem),
+        name="attend_back",
+    )(length, k_nat, v_nat, k_t, q_t, q_nat, do_t, do_nat, lse, delta)
+
+
+def contract(a, b, da, db):
+    return lax.dot_general(a, b, (((da,), (db,)), ((), ())), preferred_element_type=F32)
+
+
+def turn(v, cos_t, sin_t, sign):
+    half = HEAD_DIM // 2
+    a, b = v[:half], v[half:]
+    return jnp.concatenate([a * cos_t - sign * b * sin_t, b * cos_t + sign * a * sin_t], axis=0)
+
+
+def fast_shards(tokens, lengths, positions, w_qkv, w_out, w_in, w_down, gain_attn, gain_mlp, cotangent):
+    rows, width = tokens.shape[1], tokens.shape[2]
+    length_all = rows * CTX
+    half = width // 2
+    hidden = w_down.shape[0] * 2
+    block = hidden // 4
+    sub = block // 2
+    scale = HEAD_DIM ** (-0.5)
+    me, z, x, c = place()
+    y = lax.axis_index("shard")
+    group, pair = z // 2, (z % 2) * 2 + x
+
+    def swap(v):
+        return lax.ppermute(v, "shard", [(0, 1), (1, 0)])
+
+    def sibling(v):
+        return lax.ppermute(v, "ctx", [(i, i ^ 1) for i in range(CTX)])
+
+    def ordered(mine, other, axis):
+        return jnp.where(
+            y == 0,
+            jnp.concatenate([mine, other], axis=axis),
+            jnp.concatenate([other, mine], axis=axis),
+        )
+
+    def my_half(v, which, axis):
+        size = v.shape[axis] // 2
+        return lax.dynamic_slice_in_dim(v, which * size, size, axis)
+
+    gains = jnp.stack([gain_attn, gain_mlp])
+    gains = ordered(gains, swap(gains), 1)
+    g1, g2 = gains[0], gains[1]
+    wh = lax.dynamic_slice(w_qkv.reshape(half, 3, width), (0, 0, HEAD_DIM * me), (half, 3, HEAD_DIM))
+    wh = wh.reshape(half, 3 * HEAD_DIM).T
+    wh = ordered(wh, swap(wh), 1)
+    hidden_in = tokens[0].astype(F32)
+    h1, n1, r1 = layer_norm(hidden_in, g1)
+    hb1 = h1.astype(BF16)
+    (hb1_all, pos_all) = gather([hb1, positions.astype(F32)], 0, "gather_tokens")
+    hb1_all = hb1_all.reshape(length_all, width)
+    pos_all = pos_all.reshape(length_all)
+    hd2 = HEAD_DIM // 2
+    inverse = theta_base ** (-(jnp.arange(hd2, dtype=F32) * (2.0 / HEAD_DIM)))
+    angles = inverse[:, None] * pos_all[None, :]
+    cos_t, sin_t = jnp.cos(angles), jnp.sin(angles)
+    qkv_t = contract(wh, hb1_all, 1, 1)
+    q_t = turn(qkv_t[:HEAD_DIM], cos_t, sin_t, 1.0).astype(BF16)
+    k_t = turn(qkv_t[HEAD_DIM : 2 * HEAD_DIM], cos_t, sin_t, 1.0).astype(BF16)
+    v_t = qkv_t[2 * HEAD_DIM :].astype(BF16)
+    qs_t = q_t * jnp.asarray(scale, BF16)
+    k_nat, v_nat = k_t.T, v_t.T
+    o_t, lse = attend(lengths, k_nat, qs_t, v_t)
+    ob_h = o_t.astype(BF16)
+
+    def pieces(v):
+        return jnp.transpose(v.reshape(v.shape[0], CTX, rows), (1, 0, 2))
+
+    ob_t = exchange(pieces(ob_h), all_peers, CTX, 1, "spread_attended").reshape(width, rows)
+    w_out_all = ordered(w_out, swap(w_out), 0)
+    mid = hidden_in + contract(ob_t, w_out_all, 0, 0)
+    h2, n2, r2 = layer_norm(mid, g2)
+    hb2 = h2.astype(BF16)
+    cot_b = cotangent[0]
+    w_in3 = lax.dynamic_slice(w_in.reshape(half, 2, hidden), (0, c, block * pair), (half, 1, block))
+    w_in_half = w_in3.reshape(half, block).T
+    w_in_one = ordered(w_in_half, swap(w_in_half), 1)
+    w_in_two = sibling(w_in_one)
+    w_in_t = jnp.where(
+        c == 0, jnp.concatenate([w_in_one, w_in_two], 0), jnp.concatenate([w_in_two, w_in_one], 0)
+    )
+    owner = pair // 2
+    wd_local = lax.dynamic_slice(w_down, (block * (pair % 2) + sub * c, 0), (sub, width))
+    wd_one = jnp.where(owner == y, wd_local, swap(wd_local))
+    wd_two = sibling(wd_one)
+    wd = jnp.where(c == 0, jnp.concatenate([wd_one, wd_two], 0), jnp.concatenate([wd_two, wd_one], 0))
+    both_all = exchange(jnp.stack([hb2, cot_b]), square_peers, 4, 2, "gather_square", spread=True)
+    hb2_all = both_all[:, 0].reshape(4 * rows, width)
+    cot_all = both_all[:, 1].reshape(4 * rows, width)
+    u_t = contract(w_in_t, hb2_all, 1, 1)
+    inp, gate = u_t[:block], u_t[block:]
+    gel, dgel = gelu_parts(inp)
+    act_t = (gel * gate).astype(BF16)
+    d_act = contract(wd, cot_all, 1, 1)
+    d_u_t = jnp.concatenate([d_act * gate * dgel, d_act * gel], axis=0).astype(BF16)
+    d_h2_part = contract(d_u_t, w_in_t, 0, 0)
+    out_part = contract(act_t, wd, 0, 0)
+    parts = jnp.stack([d_h2_part, out_part]).astype(BF16).reshape(2, 4, rows, width)
+    parts = exchange(jnp.transpose(parts, (1, 0, 2, 3)), square_peers, 4, 3, "sum_square")
+    sums = jnp.sum(parts.astype(F32), axis=0)
+    d_h2 = sums[0]
+    output = (mid + sums[1]).astype(BF16)
+    gi = contract(d_u_t, hb2_all, 1, 0)
+    gd = contract(act_t, cot_all, 1, 0)
+    gi = my_half(gi, c, 0) + sibling(my_half(gi, 1 - c, 0).astype(BF16)).astype(F32)
+    gd = my_half(gd, c, 1) + sibling(my_half(gd, 1 - c, 1).astype(BF16)).astype(F32)
+    gi = my_half(gi, y, 1) + swap(my_half(gi, 1 - y, 1).astype(BF16)).astype(F32)
+    gd = gd + swap(gd.astype(BF16)).astype(F32)
+
+    def far(v):
+        return lax.ppermute(v, "ctx", [(i, (i + 8) % CTX) for i in range(CTX)])
+
+    gi = my_half(gi, group, 0) + far(my_half(gi, 1 - group, 0).astype(BF16)).astype(F32)
+    gd = my_half(gd, group, 0) + far(my_half(gd, 1 - group, 0).astype(BF16)).astype(F32)
+    gi, gd = gi.astype(BF16), gd.astype(BF16)
+    d_x2, gg2 = norm_back(d_h2, n2, r2, g2)
+    d_mid = cot_b.astype(F32) + d_x2
+    d_mid_b = d_mid.astype(BF16)
+    (d_mid_all,) = gather([d_mid_b], 4, "gather_d_mid")
+    d_mid_all = d_mid_all.reshape(length_all, width)
+    wo_h = lax.dynamic_slice(w_out_all, (HEAD_DIM * me, 0), (HEAD_DIM, width))
+    do_t = contract(wo_h, d_mid_all, 1, 1).astype(BF16)
+    delta = jnp.sum(do_t.astype(F32) * o_t, axis=0, keepdims=True)
+    dq_t, dk, dv = attend_back(lengths, k_nat, v_nat, k_t, qs_t, q_t.T, do_t, do_t.T, lse, delta)
+    dq_t = turn(dq_t * scale, cos_t, sin_t, -1.0)
+    dk_t = turn(dk.T * scale, cos_t, sin_t, -1.0)
+    d_qkv_t = jnp.concatenate([dq_t, dk_t, dv.T], axis=0).astype(BF16)
+    d_qkv = exchange(pieces(d_qkv_t), all_peers, CTX, 5, "spread_d_qkv")
+    d_qkv = jnp.transpose(d_qkv.reshape(CTX, 3, HEAD_DIM, rows), (1, 0, 2, 3)).reshape(3 * width, rows)
+    w_qkv_other = sibling(swap(my_half(w_qkv, c, 0)))
+    w_qkv_mine = swap(my_half(w_qkv, c, 0))
+    w_qkv_swap = jnp.where(
+        c == 0,
+        jnp.concatenate([w_qkv_mine, w_qkv_other], 0),
+        jnp.concatenate([w_qkv_other, w_qkv_mine], 0),
+    )
+    d_h1 = ordered(contract(d_qkv, w_qkv, 0, 1), contract(d_qkv, w_qkv_swap, 0, 1), 1)
+    d_x1, gg1 = norm_back(d_h1, n1, r1, g1)
+    grad_tokens = d_mid + d_x1
+    gq = contract(d_qkv_t, hb1_all, 1, 0)
+    go = contract(ob_h, d_mid_all, 1, 0)
+    gq = (my_half(gq, y, 1) + swap(my_half(gq, 1 - y, 1).astype(BF16)).astype(F32)).astype(BF16)
+    go = (go + swap(go.astype(BF16)).astype(F32)).astype(BF16)
+    gg = jnp.stack([gg1, gg2])
+    gg = my_half(gg, y, 1) + swap(my_half(gg, 1 - y, 1))
+    gq_all, go_all, gi_all, gd_all, gg_all = gather(
+        [gq, go, gi, gd, gg],
+        6,
+        "gather_grads",
+        (
+            everywhere,
+            lambda zo, y: zo // 2 == y,
+            everywhere,
+            lambda zo, y: zo % 2 == y,
+            everywhere,
+        ),
+    )
+    grad_qkv = jnp.transpose(gq_all.reshape(CTX, 3, HEAD_DIM, half), (3, 1, 0, 2)).reshape(half, 3 * width)
+    grad_out = lax.dynamic_slice_in_dim(go_all, y * 8, 8, 0).reshape(half, width)
+    gi_all = gi_all.reshape(2, 2, 2, 2, sub, half)
+    grad_in = jnp.transpose(gi_all, (5, 3, 1, 2, 0, 4)).reshape(half, 2 * hidden)
+    gd_all = gd_all.reshape(2, 2, 2, 2, sub, half)
+    gd_all = lax.dynamic_index_in_dim(gd_all, y, 1, keepdims=False)
+    grad_down = jnp.transpose(gd_all, (1, 0, 3, 2, 4)).reshape(hidden // 2, width)
+    gg_sum = jnp.sum(gg_all, axis=0)
+    return (
+        output.reshape(1, rows, width),
+        grad_tokens.reshape(1, rows, width),
+        grad_qkv.astype(F32),
+        grad_out.astype(F32),
+        grad_in.astype(F32),
+        grad_down.astype(F32),
+        gg_sum[0],
+        gg_sum[1],
+    )
+
+
 def solution(mesh):
     in_specs = (
         P("shard", "ctx", None),
@@ -300,4 +772,5 @@
         P("shard"),
         P("shard"),
     )
-    return jax.shard_map(shards, mesh=mesh, in_specs=in_specs, out_specs=out_specs, check_vma=False)
+    plan = fast_shards if fast_fits(mesh) else shards
+    return jax.shard_map(plan, mesh=mesh, in_specs=in_specs, out_specs=out_specs, check_vma=False)

time: 1580 us -> 511 us (0.32)
  waiting for transfers between devices: 1290 us -> 38.2 us
  Pallas kernels: 0 us -> 245 us
  blocking collectives: 89.8 us -> 0 us
  matrix products: 127 us -> 38.8 us
  local copies, waits for them, and re-layouts: 42.3 us -> 99.6 us
  other arithmetic: 10.3 us -> 52.2 us
  starting transfers between devices: 0.99 us -> 27.2 us
    reduce_scatter x4 -> x0, waiting for transfers between devices: 523 us -> none  [the longest x1 242 us: shards(): lax.psum_scatter(grad_in, 'shard', scatter_dimension=0, tiled=True)]
    all_gather x8 -> x0, waiting for transfers between devices: 388 us -> none  [the longest x1 131 us: shards(): lax.all_gather(w_in, 'shard', axis=0, tiled=True)]
    psum x1 -> x0, waiting for transfers between devices: 380 us -> none  [shards(): lax.psum((shares[0], shares[1], shares[2], shares[3], shares[4], shares[5...]
    pallas_call x0 -> x9, Pallas kernels: none -> 245 us  [the longest x3 138 us: gather(): pl.pallas_call(kernel, out_shape=[jax.ShapeDtypeStruct((CTX,) + a.shape,...]
    dot_general x19 -> x13, matrix products: 127 us -> 38.8 us  [contract(): lax.dot_general(a, b, (((da,), (db,)), ((), ())), preferred_element_type=...]
    all_gather x4 -> x0, blocking collectives: 50.2 us -> none  [the longest x1 22.8 us: shards(): lax.all_gather(lse_local, 'ctx', axis=1, tiled=True)]
    ppermute x0 -> x18, waiting for transfers between devices: none -> 38.2 us  [the longest x11 25.4 us: swap(): return lax.ppermute(v, 'shard', [(0, 1), (1, 0)])]
    psum x1 -> x0, blocking collectives: 34.5 us -> none  [shards(): lax.psum((shares[0], shares[1], shares[2], shares[3], shares[4], shares[5...]
  transfers between devices with their start and end apart: 13 -> 18, of which waited for: 12 -> 6; matrix products, arithmetic and copies ran while one was open for 9% -> 28% of each run, Pallas kernels for 0% -> 34%
where the time goes in v1:
time: 511 us; the launch traced here: 503 us
  Pallas kernels  245 us (48%)
  local copies, waits for them, and re-layouts  99.6 us (19%)
  other arithmetic  52.2 us (10%)
  matrix products  38.8 us (8%)
  waiting for transfers between devices  38.2 us (7%)
  starting transfers between devices  27.2 us (5%)
    pallas_call x3, Pallas kernels, gather(): pl.pallas_call(kernel, out_shape=[jax.ShapeDtypeStruct((CTX,) + a.shape,...  138 us
    pallas_call x4, Pallas kernels, exchange(): pl.pallas_call(functools.partial(exchange_kernel, peers, spread), out_sha...  79.1 us
    unnamed x72, local copies, waits for them, and re-layouts  46.9 us
    dot_general x13, matrix products, contract(): lax.dot_general(a, b, (((da,), (db,)), ((), ())), preferred_element_type=...  38.8 us
    ppermute x11, waiting for transfers between devices, swap(): return lax.ppermute(v, 'shard', [(0, 1), (1, 0)])  25.4 us
    another operation x4, other arithmetic  16.8 us
    pallas_call x1, Pallas kernels, attend_back(): pl.pallas_call(attend_back_kernel, out_shape=(jax.ShapeDtypeStruct((HEAD_...  15.6 us
    ppermute x11, starting transfers between devices, swap(): return lax.ppermute(v, 'shard', [(0, 1), (1, 0)])  15.1 us
  transfers between devices with their start and end apart: 18, of which 6 were waited for; matrix products, arithmetic and copies ran while one was open for 28% of the time, Pallas kernels for 34%

profile of v1, /device:TPU:0, one launch (start us, length us, event | category | flops | bytes accessed | tf_op | source)
XLA Modules:
  0.0 503.0 jit_solution(16598881213292358980)
XLA Ops:
  2.7 3.0 collective-permute-start.3
  5.7 8.3 %copy.77 = bf16[512,5248]{0,1:T(8,128)(2,1)} copy(bf16[512,5248]{1,0:T(8,128)(2,1)} %param.15) | data formatting | bytes 10747904 | tf_op args[5]
  16.0 2.1 collective-permute-start.1
  18.1 2.8 copy.66
  27.3 9.0 %collective-permute-done.1 = bf16[2,512]{1,0:T(2,128)(2,1)S(1)} collective-permute-done((bf16[2,512]{1,0:T(2,128)(2,1)S(1)}, bf16[2,512]{1,0:T(2,128)(2,1)S(1)}, u32[]{:S(2)}, u32[]{:S(2)}) %collective-permute-start.1) | collective-permute-done | bytes 2080 | tf_op jit(solution)/shard_map/ppermute | solution.py:599
  39.3 33.3 %gather_tokens.1 = (bf16[16,128,1024]{2,1,0:T(8,128)(2,1)}, f32[16,1,128]{2,1,0:T(1,128)}) custom-call(bf16[128,1024]{1,0:T(8,128)(2,1)} %fusion.54.refs_0_, f32[1,128]{1,0:T(1,128)} %convert_element_type.163.refs_1_), custom_call_target="tpu_custom_call" | custom-call | tf_op jit(solution)/shard_map/gather_tokens/pallas_call | solution.py:418
  72.6 4.1 fusion.67
  80.0 2.3 copy.111
  82.3 6.7 %fusion.34 = (bf16[32,2048]{0,1:T(8,128)(2,1)S(1)}, bf16[32,2048]{0,1:T(8,128)(2,1)S(1)}, bf16[32,2048]{0,1:T(8,128)(2,1)S(1)}, bf16[32,2048]{0,1:T(8,128)(2,1)S(1)}) fusion(f32[32,2048]{0,1:T(8,128)} %copy.111, f32[32,2048]{0,1:T(8,128)S(1)} %copy.110, f32[32]{0:T(128)S(1)} %negate_power_fusion, f32[2048]{0:T(1024)S(1)} %bitcast.201, ...), kind=kLoop, calls=%fused_computation.61 | loop fusion | flops 1114112 | bytes 1581184 | tf_op jit(solution)/shard_map/convert.35
  94.4 12.2 %attend.1 = (f32[64,2048]{1,0:T(8,128)}, f32[1,2048]{1,0:T(1,128)}) custom-call(s32[1]{0:T(128)S(6)} %copy.120.len_ref, bf16[2048,64]{1,0:T(8,128)(2,1)} %bitcast.161, bf16[64,2048]{1,0:T(8,128)(2,1)} %copy.74.q_ref, bf16[64,2048]{1,0:T(8,128)(2,1)} %copy-done.9), custom_call_target="tpu_custom_call" | custom-call | tf_op jit(solution)/shard_map/attend/pallas_call | solution.py:525
  108.4 7.4 %spread_attended.1 = bf16[16,64,128]{2,1,0:T(8,128)(2,1)} custom-call(bf16[16,64,128]{2,1,0:T(8,128)(2,1)} %bitcast_bitcast_fusion.in_ref), custom_call_target="tpu_custom_call" | custom-call | tf_op jit(solution)/shard_map/spread_attended/pallas_call | solution.py:469
  115.7 2.3 broadcast_select_fusion
  119.7 2.2 maximum_select_fusion.5
  122.0 3.0 maximum_select_fusion.3
  128.1 27.7 %gather_square.1 = bf16[4,2,128,1024]{3,2,1,0:T(8,128)(2,1)} custom-call(bf16[2,128,1024]{2,1,0:T(8,128)(2,1)} %pad_maximum_fusion.5.in_ref), custom_call_target="tpu_custom_call" | custom-call | tf_op jit(solution)/shard_map/gather_square/pallas_call | solution.py:469
  157.7 3.3 fusion.65
  161.1 3.4 fusion.28
  165.3 4.0 fusion.45
  169.3 3.6 convolution_convert_fusion.2
  172.8 2.9 convolution_convert_fusion.1
  177.3 26.9 %sum_square.1 = bf16[4,2,128,1024]{3,2,1,0:T(8,128)(2,1)} custom-call(bf16[4,2,128,1024]{3,2,1,0:T(8,128)(2,1)} %maximum_bitcast_fusion.in_ref), custom_call_target="tpu_custom_call" | custom-call | tf_op jit(solution)/shard_map/sum_square/pallas_call | solution.py:469
  204.1 2.1 convert_reduce_fusion
  208.0 29.3 %gather_d_mid.1 = bf16[16,128,1024]{2,1,0:T(8,128)(2,1)} custom-call(bf16[128,1024]{1,0:T(8,128)(2,1)} %get-tuple-element.54.refs_0_), custom_call_target="tpu_custom_call" | custom-call | tf_op jit(solution)/shard_map/gather_d_mid/pallas_call | solution.py:418
  237.3 5.1 %multiply_reduce_fusion.1 = (f32[2048]{0:T(1024)}, bf16[64,2048]{1,0:T(8,128)(2,1)}) fusion(f32[64,2048]{1,0:T(8,128)S(1)} %copy-done.5, bf16[2048,1024]{1,0:T(8,128)(2,1)} %bitcast.157, bf16[1024,1024]{1,0:T(8,128)(2,1)} %copy-done.3, s32[]{:T(128)S(6)} %select_n.157), kind=kOutput, calls=%fused_computation.111 | convolution fusion | flops 268957696 | bytes 5120004 | tf_op jit(solution)/shard_map/dot_general | solution.py:577
  246.1 15.6 %attend_back.1 = (f32[64,2048]{1,0:T(8,128)}, f32[2048,64]{1,0:T(8,128)}, f32[2048,64]{1,0:T(8,128)}) custom-call(s32[1]{0:T(128)S(6)} %copy.120.len_ref, bf16[2048,64]{1,0:T(8,128)(2,1)} %bitcast.162, bf16[2048,64]{1,0:T(8,128)(2,1)} %bitcast.181, bf16[64,2048]{1,0:T(8,128)(2,1)} %copy.79.kt_ref, bf16[64,2048]{1,0:T(8,128)(2,1)} %copy.74.q_ref, ...), custom_call_target="tpu_custom_call" | custom-call | tf_op jit(solution)/shard_map/attend_back/pallas_call | solution.py:563
  261.7 2.1 convert.81
  268.8 5.9 %fusion.44 = (bf16[32,2048]{0,1:T(8,128)(2,1)S(1)}, bf16[32,2048]{0,1:T(8,128)(2,1)}, bf16[32,2048]{0,1:T(8,128)(2,1)}, bf16[32,2048]{0,1:T(8,128)(2,1)}) fusion(f32[64,2048]{0,1:T(8,128)S(1)} %multiply_bitcast_fusion, f32[32]{0:T(128)S(1)} %negate_power_fusion, f32[2048]{0:T(1024)S(1)} %bitcast.202, f32[64,2048]{0,1:T(8,128)S(1)} %broadcast_multiply_fusion), kind=kLoop, calls=%fused_computation.71 | loop fusion | flops 1376256 | bytes 1581184 | tf_op jit(solution)/shard_map/convert.24
  291.1 17.2 %spread_d_qkv.1 = bf16[16,192,128]{2,1,0:T(8,128)(2,1)} custom-call(bf16[16,192,128]{2,1,0:T(8,128)(2,1)} %bitcast.185), custom_call_target="tpu_custom_call" | custom-call | tf_op jit(solution)/shard_map/spread_d_qkv/pallas_call | solution.py:469
  308.4 2.1 copy.92
  311.4 3.0 dynamic-slice_convert_fusion
  315.2 4.0 concatenate.105
  319.3 3.5 fusion.98
  322.7 2.3 fusion.99
  328.5 3.2 collective-permute-done.9
  335.7 3.7 fusion
  344.9 7.0 %collective-permute-done.15 = bf16[656,512]{1,0:T(8,128)(2,1)S(1)} collective-permute-done((bf16[656,512]{1,0:T(8,128)(2,1)S(1)}, bf16[656,512]{1,0:T(8,128)(2,1)S(1)}, u32[]{:S(2)}, u32[]{:S(2)}) %collective-permute-start.15) | collective-permute-done | bytes 671776 | tf_op jit(solution)/shard_map/ppermute | solution.py:599
  353.4 4.8 collective-permute-start.16
  358.2 6.1 %collective-permute-done.12 = bf16[656,512]{1,0:T(8,128)(2,1)S(1)} collective-permute-done((bf16[656,512]{1,0:T(8,128)(2,1)S(1)}, bf16[656,512]{1,0:T(8,128)(2,1)S(1)}, u32[]{:S(2)}, u32[]{:S(2)}) %collective-permute-start.12) | collective-permute-done | bytes 671776 | tf_op jit(solution)/shard_map/ppermute | solution.py:599
  364.6 4.8 collective-permute-start.13
  371.3 12.5 %collective-permute-done.13 = bf16[328,512]{1,0:T(8,128)(2,1)S(1)} collective-permute-done((bf16[328,512]{1,0:T(8,128)(2,1)S(1)}, bf16[328,512]{1,0:T(8,128)(2,1)S(1)}, u32[]{:S(2)}, u32[]{:S(2)}) %collective-permute-start.13) | collective-permute-done | bytes 335904 | tf_op jit(solution)/shard_map/ppermute | solution.py:685
  384.6 75.0 %gather_grads.1 = (bf16[16,192,512]{2,1,0:T(8,128)(2,1)}, bf16[16,64,1024]{2,1,0:T(8,128)(2,1)}, bf16[16,328,512]{2,1,0:T(8,128)(2,1)}, bf16[16,328,512]{2,1,0:T(8,128)(2,1)}, f32[16,2,512]{2,1,0:T(2,128)}) custom-call(bf16[192,512]{1,0:T(8,128)(2,1)} %add_convert_fusion.2.refs_0_, bf16[64,1024]{1,0:T(8,128)(2,1)} %add_convert_fusion.3.refs_1_, ...), custom_call_target="tpu_custom_call" | custom-call | tf_op jit(solution)/shard_map/gather_grads/pallas_call | solution.py:418
  459.6 8.2 %copy.94 = f32[2,2,2,2,328,512]{5,4,0,2,1,3:T(8,128)} copy(bf16[2,2,2,2,328,512]{5,4,3,2,1,0:T(8,128)(2,1)} %bitcast.165) | data formatting | bytes 16121856 | tf_op jit(solution)/shard_map/convert_element_type | solution.py:745
  467.8 11.8 %copy.97 = f32[512,5248]{1,0:T(8,128)} copy(f32[512,5248]{0,1:T(8,128)} %bitcast.156) | data formatting | bytes 21495808
  479.5 2.5 convert_bitcast_fusion
  482.1 4.1 copy.95
  486.2 3.8 copy.114
  490.0 3.5 copy.93
  493.5 6.7 %copy.96 = f32[512,3072]{1,0:T(8,128)} copy(f32[512,3072]{0,1:T(8,128)} %bitcast.159) | data formatting | bytes 12582912
  (164 shorter events, 80.4 us)
Async XLA Ops:
  2.7 113.0 %collective-permute-start.3 = (bf16[328,1024]{1,0:T(8,128)(2,1)}, bf16[328,1024]{1,0:T(8,128)(2,1)}, u32[]{:S(2)}, u32[]{:S(2)}) collective-permute-start(bf16[328,1024]{1,0:T(8,128)(2,1)} %constant_dynamic-slice_fusion.2), channel_id=1, source_target_pairs={{0,1},{1,0},{2,3},{3,2},{4,5},{5,4},{6,7},{7,6},{8,9},{9,8},{10,11... | collective-permute-start | bytes 2015240 | tf_op jit(solution)/shard_map/ppermute | solution.py:599
  5.7 10.3 %copy-start.24 = (bf16[512]{0:T(512)(128)(2,1)S(1)}, bf16[512]{0:T(512)(128)(2,1)}, u32[]{:S(2)}) copy-start(bf16[512]{0:T(512)(128)(2,1)} %param.17) | copy-start | bytes 3076
  5.7 10.3 %copy-start.25 = (bf16[512]{0:T(512)(128)(2,1)S(1)}, bf16[512]{0:T(512)(128)(2,1)}, u32[]{:S(2)}) copy-start(bf16[512]{0:T(512)(128)(2,1)} %param.18) | copy-start | bytes 3076
  5.7 12.4 %copy-start.1 = (bf16[512,3072]{1,0:T(8,128)(2,1)S(1)}, bf16[512,3072]{1,0:T(8,128)(2,1)}, u32[]{:S(2)}) copy-start(bf16[512,3072]{1,0:T(8,128)(2,1)} %param.13) | copy-start | bytes 9437188
  15.9 103.8 %collective-permute-start.5 = (bf16[656,512]{1,0:T(8,128)(2,1)}, bf16[656,512]{1,0:T(8,128)(2,1)}, u32[]{:S(2)}, u32[]{:S(2)}) collective-permute-start(bf16[656,512]{1,0:T(8,128)(2,1)} %dynamic-slice_bitcast_fusion), channel_id=1, source_target_pairs={{0,1},{1,0},{2,3},{3,2},{4,5},{5,4},{6,7},{7,6},{8,9},{9,8},{10,11... | collective-permute-start | bytes 2015240 | tf_op jit(solution)/shard_map/ppermute | solution.py:599
  16.0 20.3 %collective-permute-start.1 = (bf16[2,512]{1,0:T(2,128)(2,1)S(1)}, bf16[2,512]{1,0:T(2,128)(2,1)S(1)}, u32[]{:S(2)}, u32[]{:S(2)}) collective-permute-start(bf16[2,512]{1,0:T(2,128)(2,1)S(1)} %pad_maximum_fusion.6), channel_id=1, source_target_pairs={{0,1},{1,0},{2,3},{3,2},{4,5},{5,4},{6,7},{7,6},{8,9},{9,8},{10,11... | collective-permute-start | bytes 6152 | tf_op jit(solution)/shard_map/ppermute | solution.py:599
  18.1 6.5 %copy-start.2 = (bf16[1,128,1024]{2,1,0:T(8,128)(2,1)S(1)}, bf16[1,128,1024]{2,1,0:T(8,128)(2,1)}, u32[]{:S(2)}) copy-start(bf16[1,128,1024]{2,1,0:T(8,128)(2,1)} %param.10) | copy-start | bytes 786436
  20.9 5.3 %copy-start.26 = (s32[1,128]{1,0:T(1,128)S(1)}, s32[1,128]{1,0:T(1,128)}, u32[]{:S(2)}) copy-start(s32[1,128]{1,0:T(1,128)} %param.12) | copy-start | bytes 1540
  22.5 50.1 %collective-permute-start = (bf16[192,512]{1,0:T(8,128)(2,1)}, bf16[192,512]{1,0:T(8,128)(2,1)}, u32[]{:S(2)}, u32[]{:S(2)}) collective-permute-start(bf16[192,512]{1,0:T(8,128)(2,1)} %bitcast.3), channel_id=1, source_target_pairs={{0,1},{1,0},{2,3},{3,2},{4,5},{5,4},{6,7},{7,6},{8,9},{9,8},{10,11... | collective-permute-start | bytes 589832 | tf_op jit(solution)/shard_map/ppermute | solution.py:599
  22.5 99.5 %collective-permute-start.2 = (bf16[512,1024]{1,0:T(8,128)(2,1)}, bf16[512,1024]{1,0:T(8,128)(2,1)}, u32[]{:S(2)}, u32[]{:S(2)}) collective-permute-start(bf16[512,1024]{1,0:T(8,128)(2,1)} %param.14), channel_id=1, source_target_pairs={{0,1},{1,0},{2,3},{3,2},{4,5},{5,4},{6,7},{7,6},{8,9},{9,8},{10,11... | collective-permute-start | bytes 3145736 | tf_op jit(solution)/shard_map/ppermute | solution.py:599
  36.3 121.3 %collective-permute-start.7 = (bf16[256,3072]{1,0:T(8,128)(2,1)}, bf16[256,3072]{1,0:T(8,128)(2,1)}, u32[]{:S(2)}, u32[]{:S(2)}) collective-permute-start(bf16[256,3072]{1,0:T(8,128)(2,1)} %constant_dynamic-slice_fusion.1), channel_id=1, source_target_pairs={{0,1},{1,0},{2,3},{3,2},{4,5},{5,4},{6,7},{7,6},{8,9},{9,8},{10,11... | collective-permute-start | bytes 4718600 | tf_op jit(solution)/shard_map/ppermute | solution.py:599
  76.7 1.3 copy-start.13
  78.0 4.2 copy-start.23
  90.1 4.3 copy-start.9
  91.5 2.8 copy-start.4
  108.4 13.7 %copy-start.14 = (bf16[512,1024]{1,0:T(8,128)(2,1)S(1)}, bf16[512,1024]{1,0:T(8,128)(2,1)}, u32[]{:S(2)}) copy-start(bf16[512,1024]{1,0:T(8,128)(2,1)} %param.14) | copy-start | bytes 3145732
  118.0 43.0 %collective-permute-start.4 = (bf16[328,1024]{1,0:T(8,128)(2,1)}, bf16[328,1024]{1,0:T(8,128)(2,1)}, u32[]{:S(2)}, u32[]{:S(2)}) collective-permute-start(bf16[328,1024]{1,0:T(8,128)(2,1)} %broadcast_select_fusion), channel_id=1, source_target_pairs={{0,2},{2,0},{4,6},{6,4},{8,10},{10,8},{12,14},{14,12},{16,18},{18,... | collective-permute-start | bytes 2015240 | tf_op jit(solution)/shard_map/ppermute | solution.py:602
  121.9 35.8 %copy-start.11 = (bf16[656,1024]{1,0:T(8,128)(2,1)}, bf16[656,1024]{1,0:T(8,128)(2,1)S(1)}, u32[]{:S(2)}) copy-start(bf16[656,1024]{1,0:T(8,128)(2,1)S(1)} %maximum_select_fusion.5) | copy-start | bytes 4030468
  121.9 4.4 copy-start.19
  121.9 35.8 %collective-permute-start.6 = (bf16[656,1024]{1,0:T(8,128)(2,1)S(1)}, bf16[656,1024]{1,0:T(8,128)(2,1)}, u32[]{:S(2)}, u32[]{:S(2)}) collective-permute-start(bf16[656,1024]{1,0:T(8,128)(2,1)S(1)} %maximum_select_fusion.5), channel_id=1, source_target_pairs={{0,2},{2,0},{4,6},{6,4},{8,10},{10,8},{12,14},{14,12},{16,18},{18,... | collective-permute-start | bytes 4030472 | tf_op jit(solution)/shard_map/ppermute | solution.py:602
  125.0 1.3 copy-start.3
  125.0 2.2 copy-start.17
  157.6 178.1 %collective-permute-start.8 = (bf16[256,3072]{1,0:T(8,128)(2,1)}, bf16[256,3072]{1,0:T(8,128)(2,1)}, u32[]{:S(2)}, u32[]{:S(2)}) collective-permute-start(bf16[256,3072]{1,0:T(8,128)(2,1)} %collective-permute-done.7), channel_id=1, source_target_pairs={{0,2},{2,0},{4,6},{6,4},{8,10},{10,8},{12,14},{14,12},{16,18},{18,... | collective-permute-start | bytes 4718600 | tf_op jit(solution)/shard_map/ppermute | solution.py:602
  165.3 4.0 copy-start.12
  204.1 2.6 copy-start.18
  208.0 29.3 %copy-start.5 = (f32[64,2048]{1,0:T(8,128)S(1)}, f32[64,2048]{1,0:T(8,128)}, u32[]{:S(2)}) copy-start(f32[64,2048]{1,0:T(8,128)} %get-tuple-element.22) | copy-start | bytes 1572868
  237.3 5.1 %copy-start = (bf16[16,128,1024]{2,1,0:T(8,128)(2,1)S(1)}, bf16[16,128,1024]{2,1,0:T(8,128)(2,1)}, u32[]{:S(2)}) copy-start(bf16[16,128,1024]{2,1,0:T(8,128)(2,1)} %gather_d_mid.1) | copy-start | bytes 12582916
  261.7 4.2 copy-start.20
  267.2 1.5 copy-start.16
  311.4 21.0 %collective-permute-start.14 = (bf16[656,512]{1,0:T(8,128)(2,1)}, bf16[656,512]{1,0:T(8,128)(2,1)}, u32[]{:S(2)}, u32[]{:S(2)}) collective-permute-start(bf16[656,512]{1,0:T(8,128)(2,1)} %dynamic-slice_convert_fusion.1), channel_id=1, source_target_pairs={{0,2},{2,0},{4,6},{6,4},{8,10},{10,8},{12,14},{14,12},{16,18},{18,... | collective-permute-start | bytes 2015240 | tf_op jit(solution)/shard_map/ppermute | solution.py:602
  314.4 25.6 %collective-permute-start.11 = (bf16[656,1024]{1,0:T(8,128)(2,1)}, bf16[656,1024]{1,0:T(8,128)(2,1)}, u32[]{:S(2)}, u32[]{:S(2)}) collective-permute-start(bf16[656,1024]{1,0:T(8,128)(2,1)} %dynamic-slice_convert_fusion), channel_id=1, source_target_pairs={{0,2},{2,0},{4,6},{6,4},{8,10},{10,8},{12,14},{14,12},{16,18},{18,... | collective-permute-start | bytes 4030472 | tf_op jit(solution)/shard_map/ppermute | solution.py:602
  314.9 12.0 %collective-permute-start.10 = (bf16[64,1024]{1,0:T(8,128)(2,1)}, bf16[64,1024]{1,0:T(8,128)(2,1)}, u32[]{:S(2)}, u32[]{:S(2)}) collective-permute-start(bf16[64,1024]{1,0:T(8,128)(2,1)} %get-tuple-element.88), channel_id=1, source_target_pairs={{0,1},{1,0},{2,3},{3,2},{4,5},{5,4},{6,7},{7,6},{8,9},{9,8},{10,11... | collective-permute-start | bytes 393224 | tf_op jit(solution)/shard_map/ppermute | solution.py:599
  319.3 3.5 copy-start.6
  322.7 4.2 copy-start.15
  325.0 10.7 %copy-start.7 = (bf16[16,3,64,128]{3,2,0,1:T(8,128)(2,1)S(1)}, bf16[16,3,64,128]{3,2,0,1:T(8,128)(2,1)}, u32[]{:S(2)}) copy-start(bf16[16,3,64,128]{3,2,0,1:T(8,128)(2,1)} %copy.92) | copy-start | bytes 2359300
  325.1 6.6 %collective-permute-start.9 = (bf16[192,512]{1,0:T(8,128)(2,1)S(1)}, bf16[192,512]{1,0:T(8,128)(2,1)S(1)}, u32[]{:S(2)}, u32[]{:S(2)}) collective-permute-start(bf16[192,512]{1,0:T(8,128)(2,1)S(1)} %dynamic-slice_convert_fusion.5), channel_id=1, source_target_pairs={{0,1},{1,0},{2,3},{3,2},{4,5},{5,4},{6,7},{7,6},{8,9},{9,8},{10,11... | collective-permute-start | bytes 589832 | tf_op jit(solution)/shard_map/ppermute | solution.py:599
  332.4 7.6 %slice-start = ((s8[5373952]{0:T(1024)(128)(4,1)}), s8[4194304]{0:T(1024)(128)(4,1)S(1)}, s32[]{:S(2)}) async-start(s8[5373952]{0:T(1024)(128)(4,1)} %bitcast.179), calls=%async_computation | async-start | bytes 8388608
  333.9 6.2 %slice-start.1 = ((s8[5373952]{0:T(1024)(128)(4,1)}), s8[1179648]{0:T(1024)(128)(4,1)S(1)}, s32[]{:S(2)}) async-start(s8[5373952]{0:T(1024)(128)(4,1)} %bitcast.179), calls=%async_computation.1 | async-start | bytes 2359296
  333.9 18.0 %collective-permute-start.15 = (bf16[656,512]{1,0:T(8,128)(2,1)S(1)}, bf16[656,512]{1,0:T(8,128)(2,1)S(1)}, u32[]{:S(2)}, u32[]{:S(2)}) collective-permute-start(bf16[656,512]{1,0:T(8,128)(2,1)S(1)} %fusion.46), channel_id=1, source_target_pairs={{0,1},{1,0},{2,3},{3,2},{4,5},{5,4},{6,7},{7,6},{8,9},{9,8},{10,11... | collective-permute-start | bytes 2015240 | tf_op jit(solution)/shard_map/ppermute | solution.py:599
  339.7 29.7 %collective-permute-start.17 = (f32[2,512]{1,0:T(2,128)S(1)}, f32[2,512]{1,0:T(2,128)S(1)}, u32[]{:S(2)}, u32[]{:S(2)}) collective-permute-start(f32[2,512]{1,0:T(2,128)S(1)} %fusion.82), channel_id=1, source_target_pairs={{0,1},{1,0},{2,3},{3,2},{4,5},{5,4},{6,7},{7,6},{8,9},{9,8},{10,11... | collective-permute-start | bytes 12296 | tf_op jit(solution)/shard_map/ppermute | solution.py:599
  340.0 3.8 copy-start.10
  342.0 22.3 %collective-permute-start.12 = (bf16[656,512]{1,0:T(8,128)(2,1)S(1)}, bf16[656,512]{1,0:T(8,128)(2,1)S(1)}, u32[]{:S(2)}, u32[]{:S(2)}) collective-permute-start(bf16[656,512]{1,0:T(8,128)(2,1)S(1)} %dynamic-slice_convert_fusion.2), channel_id=1, source_target_pairs={{0,1},{1,0},{2,3},{3,2},{4,5},{5,4},{6,7},{7,6},{8,9},{9,8},{10,11... | collective-permute-start | bytes 2015240 | tf_op jit(solution)/shard_map/ppermute | solution.py:599
  353.4 17.1 %collective-permute-start.16 = (bf16[328,512]{1,0:T(8,128)(2,1)S(1)}, bf16[328,512]{1,0:T(8,128)(2,1)S(1)}, u32[]{:S(2)}, u32[]{:S(2)}) collective-permute-start(bf16[328,512]{1,0:T(8,128)(2,1)S(1)} %dynamic-slice_convert_fusion.3), channel_id=1, source_target_pairs={{0,16},{2,18},{4,20},{6,22},{8,24},{10,26},{12,28},{14,30},{16,0},... | collective-permute-start | bytes 1007624 | tf_op jit(solution)/shard_map/ppermute | solution.py:685
  364.6 19.2 %collective-permute-start.13 = (bf16[328,512]{1,0:T(8,128)(2,1)S(1)}, bf16[328,512]{1,0:T(8,128)(2,1)S(1)}, u32[]{:S(2)}, u32[]{:S(2)}) collective-permute-start(bf16[328,512]{1,0:T(8,128)(2,1)S(1)} %dynamic-slice_convert_fusion.4), channel_id=1, source_target_pairs={{0,16},{2,18},{4,20},{6,22},{8,24},{10,26},{12,28},{14,30},{16,0},... | collective-permute-start | bytes 1007624 | tf_op jit(solution)/shard_map/ppermute | solution.py:685
  486.2 3.8 copy-start.8
  493.5 6.7 %copy-start.21 = (bf16[16,64,1024]{2,1,0:T(8,128)(2,1)S(1)}, bf16[16,64,1024]{2,1,0:T(8,128)(2,1)}, u32[]{:S(2)}) copy-start(bf16[16,64,1024]{2,1,0:T(8,128)(2,1)} %get-tuple-element.28) | copy-start | bytes 6291460
  500.2 1.7 copy-start.22
